TPU v7x, 32 devices: a whole 2x2x4 slice. The times are simulated.
32 devices in a mesh: section: 2 (over x), expert: 4 (over y, core), dp: 4 (over z).
Axes of the slice: x: 2, y: 2, z: 4, core: 2. Of those that a mesh axis runs over, the one named last changes fastest.
Arguments:
- arrivals: bfloat16 [2, 1024, 2048], P('section', ('expert', 'dp')), may hold values from -6 to 6
- fresh: bfloat16 [1, 1024, 2048], P(None, ('expert', 'dp')), may hold values from -6 to 6
- routes: int32 [2, 2, 1024, 6], P('section', None, ('expert', 'dp')), may hold values from 0 to 63, as said below
- gates: bfloat16 [2, 2, 1024, 6], P('section', None, ('expert', 'dp')), may hold values from 0.099609375 to 1
- cotangent: bfloat16 [2, 2, 1024, 2048], P('section', None, ('expert', 'dp')), may hold values from -0.3125 to 0.3125
- norm_gain: float32 [2, 2048], P('section'), may hold values from 0.5 to 1.5
- w_gate: bfloat16 [2, 1408, 2048], P('section', 'expert', 'dp'), may hold values from -0.125 to 0.125
- w_up: bfloat16 [2, 1408, 2048], P('section', 'expert', 'dp'), may hold values from -0.125 to 0.125
- w_down: bfloat16 [2, 1408, 2048], P('section', 'expert', 'dp'), may hold values from -0.15625 to 0.15625
Outputs:
- layer_out: bfloat16 [2, 2, 1024, 2048], P('section', None, ('expert', 'dp'))
- grad_down: float32 [2, 1408, 2048], P('section', 'expert', 'dp')
Inputs may be any that keep to these rules, and one draw needn't show every extreme that they name: `routes`: each token's 6 entries are different expert numbers.
All inputs are finite; a program needn't handle non-finite values.
Results may differ from a plain program's by a relative error of at most 0.0085.
Values may be sent and summed in bfloat16 or wider, within the bound.
A program may use at most 64 MiB of HBM per device.

v0:
```python
import jax
import jax.numpy as jnp
from jax import lax
from jax.sharding import PartitionSpec as P

SPLIT = 4
CAP = 12


def shifted_2(shard, axis, by):
    count = lax.axis_size(axis)
    pairs = [(i, i + by) for i in range(count) if 0 <= i + by < count]
    return lax.ppermute(shard, axis, pairs)


def local(arrivals, fresh, routes, gates, cotangent, norm_gain, w_gate, w_up, w_down):
    n_expert = lax.axis_size("expert")
    flight = n_expert // SPLIT
    section_index = lax.axis_index("section")
    tok_rows = arrivals.shape[1]
    model_width = arrivals.shape[2]
    step_count = routes.shape[1]
    gains = norm_gain[0]
    gate_local, up_local, down_local = (
        lax.all_gather(w_gate[0], "dp", axis=1, tiled=True),
        lax.all_gather(w_up[0], "dp", axis=1, tiled=True),
        lax.all_gather(w_down[0], "dp", axis=1, tiled=True),
    )
    hid_rows = gate_local.shape[0]
    slot_ids = jnp.arange(CAP, dtype=jnp.int32)
    expert_ids = jnp.arange(flight, dtype=jnp.int32)
    highest = lax.Precision.HIGHEST
    row_dims = (((0,), (0,)), ((), ()))

    def selection(step_index):
        routing = routes[0, step_index]
        weights = gates[0, step_index].astype(jnp.float32)
        matches = routing[:, :, None] == expert_ids[None, None, :]
        naming = jnp.any(matches, axis=1).astype(jnp.int32)
        shares = jnp.sum(jnp.where(matches, weights[:, :, None], 0.0), axis=1)
        places = jnp.cumsum(naming, axis=0) - naming
        chosen = (naming.T[:, None, :] == 1) & (places.T[:, None, :] == slot_ids[None, :, None])
        select = chosen.reshape(flight * CAP, tok_rows).astype(jnp.bfloat16)
        slot_gate = jnp.sum(jnp.where(chosen, shares.T[:, None, :], 0.0), axis=2).reshape(
            flight * CAP
        )
        counts = jnp.minimum(jnp.sum(naming, axis=0), CAP)
        return (select, slot_gate, counts)

    def fan_out(block_in):
        spread = jnp.broadcast_to(block_in[:, None], (flight, SPLIT) + block_in.shape[1:])
        return spread.reshape((n_expert,) + block_in.shape[1:])

    def pack_rows(select, values):
        rows = jnp.dot(select, values, preferred_element_type=jnp.float32).astype(jnp.bfloat16)
        return fan_out(rows.reshape(flight, CAP, model_width))

    picks = [selection(turn_num) for turn_num in range(step_count)]
    incoming = arrivals[0]
    grad_total = jnp.zeros((hid_rows, model_width), jnp.float32)
    outputs = []
    for turn_num in range(step_count):
        if turn_num > 0:
            shifted = shifted_2(outputs[-1], "section", 1)
            incoming = jnp.where(section_index == 0, fresh[turn_num - 1], shifted)
        floats = incoming.astype(jnp.float32)
        scale = lax.rsqrt(jnp.mean(floats * floats, axis=1, keepdims=True) + 0.5)
        normed = (floats * scale * gains[None, :]).astype(jnp.bfloat16)
        select, slot_gate, counts = picks[turn_num]
        send_tok = pack_rows(select, normed)
        send_cot = pack_rows(select, cotangent[0, turn_num])
        send_gate = fan_out(slot_gate.reshape(flight, CAP).astype(jnp.bfloat16))
        send_count = fan_out(counts)
        rows_tok, rows_cot, rows_gate, rows_count = (
            lax.all_to_all(send_tok, "expert", split_axis=0, concat_axis=0, tiled=True),
            lax.all_to_all(send_cot, "expert", split_axis=0, concat_axis=0, tiled=True),
            lax.all_to_all(send_gate, "expert", split_axis=0, concat_axis=0, tiled=True),
            lax.all_to_all(send_count, "expert", split_axis=0, concat_axis=0, tiled=True),
        )
        total_rows = n_expert * CAP
        flat_tok = rows_tok.reshape(total_rows, model_width)
        flat_cot = rows_cot.reshape(total_rows, model_width)
        flat_gate = rows_gate.reshape(total_rows)
        dims = (((1,), (1,)), ((), ()))
        gate_act = lax.dot_general(flat_tok, gate_local, dims, preferred_element_type=jnp.float32)
        up_act = lax.dot_general(flat_tok, up_local, dims, preferred_element_type=jnp.float32)
        hidden = (jax.nn.silu(gate_act) * up_act).astype(jnp.bfloat16)
        partial_value = jnp.dot(hidden, down_local, preferred_element_type=jnp.float32).astype(
            jnp.bfloat16
        )
        weighted = (hidden.astype(jnp.float32) * flat_gate.astype(jnp.float32)[:, None]).astype(
            jnp.bfloat16
        )
        expert_partial_value = partial_value
        grad_add = lax.dot_general(weighted, flat_cot, row_dims, preferred_element_type=jnp.float32)
        partial_value, grad_add = (
            expert_partial_value.reshape(n_expert, CAP, model_width),
            grad_add,
        )
        returned = lax.all_to_all(partial_value, "expert", split_axis=0, concat_axis=0, tiled=True)
        expert_out = jnp.sum(
            returned.reshape(flight, SPLIT, CAP, model_width).astype(jnp.float32), axis=1
        ).reshape(flight * CAP, model_width)
        mixing = select.astype(jnp.float32).T * slot_gate[None, :]
        mixture = jnp.dot(mixing, expert_out, precision=highest)
        result = (floats + mixture).astype(jnp.bfloat16)
        outputs.append(result)
        grad_total = grad_total + grad_add
    grad_part = lax.psum_scatter(grad_total, "dp", scatter_dimension=1, tiled=True)
    return (jnp.stack(outputs)[None], grad_part[None])


def solution(mesh):
    placed = (
        P("section", ("expert", "dp"), None),
        P(None, ("expert", "dp"), None),
        P("section", None, ("expert", "dp"), None),
        P("section", None, ("expert", "dp"), None),
        P("section", None, ("expert", "dp"), None),
        P("section", None),
        P("section", "expert", "dp"),
        P("section", "expert", "dp"),
        P("section", "expert", "dp"),
    )
    return jax.shard_map(
        local,
        mesh=mesh,
        in_specs=placed,
        out_specs=(P("section", None, ("expert", "dp"), None), P("section", "expert", "dp")),
        check_vma=False,
    )
```

profile of v0, /device:TPU:0, one launch (start us, length us, event | category | flops | bytes accessed | tf_op | source)
XLA Modules:
  0.0 242.2 jit_solution(11923948752257591277)
XLA Ops:
  12.7 4.3 %all-to-all-start = ((bf16[4,12,2048]{2,1,0:T(8,128)(2,1)}), bf16[4,12,2048]{2,1,0:T(8,128)(2,1)S(1)}, u32[]{:S(2)}, u32[]{:S(2)}) async-start(bf16[4,12,2048]{2,1,0:T(8,128)(2,1)} %reshape.550), calls=%async_computation | async-start | bytes 524288 | tf_op jit(solution)/shard_map/all_to_all | solution.py:75
  17.7 5.3 %all-to-all-done = bf16[4,12,2048]{2,1,0:T(8,128)(2,1)S(1)} async-done(((bf16[4,12,2048]{2,1,0:T(8,128)(2,1)}), bf16[4,12,2048]{2,1,0:T(8,128)(2,1)S(1)}, u32[]{:S(2)}, u32[]{:S(2)}) %all-to-all-start) | async-done | bytes 196640 | tf_op jit(solution)/shard_map/all_to_all | solution.py:75
  23.0 24.1 %all-gather.7.cloned.1.call-done = bf16[1,352,2048]{2,1,0:T(8,128)(2,1)} async-done(((bf16[1,352,512]{2,1,0:T(8,128)(2,1)}), bf16[1,352,2048]{2,1,0:T(8,128)(2,1)}) %all-gather.7.cloned.1.call-update) | async-done | bytes 1441808 | tf_op jit(solution)/shard_map/all_gather | solution.py:25
  47.0 1.9 fusion.11
  49.0 33.5 %all-gather.9.cloned.1.call-done = bf16[1,352,2048]{2,1,0:T(8,128)(2,1)} async-done(((bf16[1,352,512]{2,1,0:T(8,128)(2,1)}), bf16[1,352,2048]{2,1,0:T(8,128)(2,1)}) %all-gather.9.cloned.1.call-update) | async-done | bytes 1441808 | tf_op jit(solution)/shard_map/all_gather | solution.py:26
  82.5 1.9 fusion.22
  84.4 33.4 %all-gather.11.cloned.1.call-done = bf16[1,352,2048]{2,1,0:T(8,128)(2,1)} async-done(((bf16[1,352,512]{2,1,0:T(8,128)(2,1)}), bf16[1,352,2048]{2,1,0:T(8,128)(2,1)}) %all-gather.11.cloned.1.call-update) | async-done | bytes 1441808 | tf_op jit(solution)/shard_map/all_gather | solution.py:27
  117.8 1.7 convolution_convert_fusion.1
  120.3 3.4 %all-to-all-start.1 = ((bf16[4,12,2048]{2,1,0:T(8,128)(2,1)}), bf16[4,12,2048]{2,1,0:T(8,128)(2,1)S(1)}, u32[]{:S(2)}, u32[]{:S(2)}) async-start(bf16[4,12,2048]{2,1,0:T(8,128)(2,1)} %reshape.552), calls=%async_computation.1 | async-start | bytes 524288 | tf_op jit(solution)/shard_map/all_to_all | solution.py:100
  123.9 5.8 %all-to-all-done.1 = bf16[4,12,2048]{2,1,0:T(8,128)(2,1)S(1)} async-done(((bf16[4,12,2048]{2,1,0:T(8,128)(2,1)}), bf16[4,12,2048]{2,1,0:T(8,128)(2,1)S(1)}, u32[]{:S(2)}, u32[]{:S(2)}) %all-to-all-start.1) | async-done | bytes 196640 | tf_op jit(solution)/shard_map/all_to_all | solution.py:100
  130.3 3.2 %all-to-all-start.4 = ((bf16[4,1,12]{2,1,0:T(2,128)(2,1)}), bf16[4,1,12]{2,1,0:T(2,128)(2,1)S(1)}, u32[]{:S(2)}, u32[]{:S(2)}) async-start(bf16[4,1,12]{2,1,0:T(2,128)(2,1)} %reshape.557), calls=%async_computation.4 | async-start | bytes 4096 | tf_op jit(solution)/shard_map/all_to_all | solution.py:77
  134.2 3.0 %all-to-all-done.4 = bf16[4,1,12]{2,1,0:T(2,128)(2,1)S(1)} async-done(((bf16[4,1,12]{2,1,0:T(2,128)(2,1)}), bf16[4,1,12]{2,1,0:T(2,128)(2,1)S(1)}, u32[]{:S(2)}, u32[]{:S(2)}) %all-to-all-start.4) | async-done | bytes 128 | tf_op jit(solution)/shard_map/all_to_all | solution.py:77
  137.8 3.2 %all-to-all-start.6 = ((bf16[4,1,12]{2,1,0:T(2,128)(2,1)}), bf16[4,1,12]{2,1,0:T(2,128)(2,1)S(1)}, u32[]{:S(2)}, u32[]{:S(2)}) async-start(bf16[4,1,12]{2,1,0:T(2,128)(2,1)} %reshape.560), calls=%async_computation.6 | async-start | bytes 4096 | tf_op jit(solution)/shard_map/all_to_all | solution.py:77
  141.0 3.5 %collective-permute-start = (bf16[64,2048]{1,0:T(8,128)(2,1)S(1)}, bf16[64,2048]{1,0:T(8,128)(2,1)S(1)}, u32[]{:S(2)}, u32[]{:S(2)}) collective-permute-start(bf16[64,2048]{1,0:T(8,128)(2,1)S(1)} %fusion), channel_id=1, source_target_pairs={{0,16},{1,17},{2,18},{3,19},{4,20},{5,21},{6,22},{7,23},{8,24},{9,... | collective-permute-start | bytes 786440 | tf_op jit(solution)/shard_map/ppermute | solution.py:13
  145.4 3.4 %all-to-all-start.5 = ((bf16[4,12,2048]{2,1,0:T(8,128)(2,1)}), bf16[4,12,2048]{2,1,0:T(8,128)(2,1)S(1)}, u32[]{:S(2)}, u32[]{:S(2)}) async-start(bf16[4,12,2048]{2,1,0:T(8,128)(2,1)} %reshape.558), calls=%async_computation.5 | async-start | bytes 524288 | tf_op jit(solution)/shard_map/all_to_all | solution.py:76
  149.0 5.8 %all-to-all-done.5 = bf16[4,12,2048]{2,1,0:T(8,128)(2,1)S(1)} async-done(((bf16[4,12,2048]{2,1,0:T(8,128)(2,1)}), bf16[4,12,2048]{2,1,0:T(8,128)(2,1)S(1)}, u32[]{:S(2)}, u32[]{:S(2)}) %all-to-all-start.5) | async-done | bytes 196640 | tf_op jit(solution)/shard_map/all_to_all | solution.py:76
  155.5 3.4 %all-to-all-start.7 = ((bf16[4,12,2048]{2,1,0:T(8,128)(2,1)}), bf16[4,12,2048]{2,1,0:T(8,128)(2,1)S(1)}, u32[]{:S(2)}, u32[]{:S(2)}) async-start(bf16[4,12,2048]{2,1,0:T(8,128)(2,1)} %reshape.561), calls=%async_computation.7 | async-start | bytes 524288 | tf_op jit(solution)/shard_map/all_to_all | solution.py:76
  159.8 5.1 %all-to-all-done.7 = bf16[4,12,2048]{2,1,0:T(8,128)(2,1)S(1)} async-done(((bf16[4,12,2048]{2,1,0:T(8,128)(2,1)}), bf16[4,12,2048]{2,1,0:T(8,128)(2,1)S(1)}, u32[]{:S(2)}, u32[]{:S(2)}) %all-to-all-start.7) | async-done | bytes 196640 | tf_op jit(solution)/shard_map/all_to_all | solution.py:76
  166.8 3.4 %all-to-all-start.2 = ((bf16[4,12,2048]{2,1,0:T(8,128)(2,1)}), bf16[4,12,2048]{2,1,0:T(8,128)(2,1)S(1)}, u32[]{:S(2)}, u32[]{:S(2)}) async-start(bf16[4,12,2048]{2,1,0:T(8,128)(2,1)} %reshape.554), calls=%async_computation.2 | async-start | bytes 524288 | tf_op jit(solution)/shard_map/all_to_all | solution.py:75
  171.7 4.5 %all-to-all-done.2 = bf16[4,12,2048]{2,1,0:T(8,128)(2,1)S(1)} async-done(((bf16[4,12,2048]{2,1,0:T(8,128)(2,1)}), bf16[4,12,2048]{2,1,0:T(8,128)(2,1)S(1)}, u32[]{:S(2)}, u32[]{:S(2)}) %all-to-all-start.2) | async-done | bytes 196640 | tf_op jit(solution)/shard_map/all_to_all | solution.py:75
  176.3 2.0 fusion.9
  178.9 2.2 convolution_add_fusion
  182.9 8.4 %all_to_all.42 = bf16[4,12,2048]{2,1,0:T(8,128)(2,1)S(1)} all-to-all(bf16[4,12,2048]{2,1,0:T(8,128)(2,1)S(1)} %reshape.556), channel_id=1, replica_groups=mesh['section'=2,'expert'=4,'dp'=4] {'expert'}, dimensions={0} | all-to-all | bytes 393216 | tf_op jit(solution)/shard_map/all_to_all | solution.py:100
  192.9 42.8 %reduce-scatter.2.cloned.1.call-done = f32[352,512]{1,0:T(8,128)} async-done(((f32[352,2048]{1,0:T(8,128)}), f32[352,512]{1,0:T(8,128)}) %reduce-scatter.2.cloned.1.call-update) | async-done | bytes 720912 | tf_op jit(solution)/shard_map/reduce_scatter | solution.py:109
  (86 shorter events, 18.7 us)
Async XLA Ops:
  7.2 10.1 %copy-start.10 = (s32[1,2,64,6]{2,1,3,0:T(2,128)S(1)}, s32[1,2,64,6]{2,1,3,0:T(2,128)}, u32[]{:S(2)}) copy-start(s32[1,2,64,6]{2,1,3,0:T(2,128)} %param.11) | copy-start | bytes 9220
  7.2 4.5 %copy-start.2 = (bf16[1,64,2048]{2,1,0:T(8,128)(2,1)S(1)}, bf16[1,64,2048]{2,1,0:T(8,128)(2,1)}, u32[]{:S(2)}) copy-start(bf16[1,64,2048]{2,1,0:T(8,128)(2,1)} %param.9) | copy-start | bytes 786436
  7.2 4.5 %copy-start.13 = (f32[1,2048]{1,0:T(1,128)S(1)}, f32[1,2048]{1,0:T(1,128)}, u32[]{:S(2)}) copy-start(f32[1,2048]{1,0:T(1,128)} %param.14) | copy-start | bytes 24580
  7.2 10.1 %copy-start.11 = (bf16[1,2,64,6]{2,1,3,0:T(2,128)(2,1)S(1)}, bf16[1,2,64,6]{2,1,3,0:T(2,128)(2,1)}, u32[]{:S(2)}) copy-start(bf16[1,2,64,6]{2,1,3,0:T(2,128)(2,1)} %param.12) | copy-start | bytes 4612
  7.2 39.8 %all-gather.7.cloned.1.call-start = ((), (), s32[]{:S(2)}) async-start(), calls=%async_computation.10 | async-start | bytes 1802240 | tf_op jit(solution)/shard_map/all_gather | solution.py:25
  7.9 74.5 %all-gather.9.cloned.1.call-start = ((), (), s32[]{:S(2)}) async-start(), calls=%async_computation.11 | async-start | bytes 1802240 | tf_op jit(solution)/shard_map/all_gather | solution.py:26
  8.7 109.1 %all-gather.11.cloned.1.call-start = ((), (), s32[]{:S(2)}) async-start(), calls=%async_computation.12 | async-start | bytes 1802240 | tf_op jit(solution)/shard_map/all_gather | solution.py:27
  12.7 10.3 %all-to-all-start = ((bf16[4,12,2048]{2,1,0:T(8,128)(2,1)}), bf16[4,12,2048]{2,1,0:T(8,128)(2,1)S(1)}, u32[]{:S(2)}, u32[]{:S(2)}) async-start(bf16[4,12,2048]{2,1,0:T(8,128)(2,1)} %reshape.550), calls=%async_computation | async-start | bytes 524288 | tf_op jit(solution)/shard_map/all_to_all | solution.py:75
  84.4 35.9 %copy-start.8 = (bf16[48,352]{1,0:T(8,128)(2,1)}, bf16[48,352]{1,0:T(8,128)(2,1)S(1)}, u32[]{:S(2)}) copy-start(bf16[48,352]{1,0:T(8,128)(2,1)S(1)} %fusion.22) | copy-start | bytes 101380
  84.4 39.3 %copy-start.7 = (bf16[1,2,64,2048]{3,2,1,0:T(8,128)(2,1)S(1)}, bf16[1,2,64,2048]{3,2,1,0:T(8,128)(2,1)}, u32[]{:S(2)}) copy-start(bf16[1,2,64,2048]{3,2,1,0:T(8,128)(2,1)} %param.13) | copy-start | bytes 1572868
  120.3 9.4 %all-to-all-start.1 = ((bf16[4,12,2048]{2,1,0:T(8,128)(2,1)}), bf16[4,12,2048]{2,1,0:T(8,128)(2,1)S(1)}, u32[]{:S(2)}, u32[]{:S(2)}) async-start(bf16[4,12,2048]{2,1,0:T(8,128)(2,1)} %reshape.552), calls=%async_computation.1 | async-start | bytes 524288 | tf_op jit(solution)/shard_map/all_to_all | solution.py:100
  130.3 6.9 %all-to-all-start.4 = ((bf16[4,1,12]{2,1,0:T(2,128)(2,1)}), bf16[4,1,12]{2,1,0:T(2,128)(2,1)S(1)}, u32[]{:S(2)}, u32[]{:S(2)}) async-start(bf16[4,1,12]{2,1,0:T(2,128)(2,1)} %reshape.557), calls=%async_computation.4 | async-start | bytes 4096 | tf_op jit(solution)/shard_map/all_to_all | solution.py:77
  134.2 30.7 %copy-start.5 = (bf16[64,2048]{1,0:T(8,128)(2,1)}, bf16[64,2048]{1,0:T(8,128)(2,1)S(1)}, u32[]{:S(2)}) copy-start(bf16[64,2048]{1,0:T(8,128)(2,1)S(1)} %fusion) | copy-start | bytes 786436
  137.8 6.9 %all-to-all-start.6 = ((bf16[4,1,12]{2,1,0:T(2,128)(2,1)}), bf16[4,1,12]{2,1,0:T(2,128)(2,1)S(1)}, u32[]{:S(2)}, u32[]{:S(2)}) async-start(bf16[4,1,12]{2,1,0:T(2,128)(2,1)} %reshape.560), calls=%async_computation.6 | async-start | bytes 4096 | tf_op jit(solution)/shard_map/all_to_all | solution.py:77
  141.0 24.0 %copy-start.9 = (bf16[1,64,2048]{2,1,0:T(8,128)(2,1)S(1)}, bf16[1,64,2048]{2,1,0:T(8,128)(2,1)}, u32[]{:S(2)}) copy-start(bf16[1,64,2048]{2,1,0:T(8,128)(2,1)} %param.10) | copy-start | bytes 786436
  141.0 23.9 %collective-permute-start = (bf16[64,2048]{1,0:T(8,128)(2,1)S(1)}, bf16[64,2048]{1,0:T(8,128)(2,1)S(1)}, u32[]{:S(2)}, u32[]{:S(2)}) collective-permute-start(bf16[64,2048]{1,0:T(8,128)(2,1)S(1)} %fusion), channel_id=1, source_target_pairs={{0,16},{1,17},{2,18},{3,19},{4,20},{5,21},{6,22},{7,23},{8,24},{9,... | collective-permute-start | bytes 786440 | tf_op jit(solution)/shard_map/ppermute | solution.py:13
  145.4 9.4 %all-to-all-start.5 = ((bf16[4,12,2048]{2,1,0:T(8,128)(2,1)}), bf16[4,12,2048]{2,1,0:T(8,128)(2,1)S(1)}, u32[]{:S(2)}, u32[]{:S(2)}) async-start(bf16[4,12,2048]{2,1,0:T(8,128)(2,1)} %reshape.558), calls=%async_computation.5 | async-start | bytes 524288 | tf_op jit(solution)/shard_map/all_to_all | solution.py:76
  155.5 9.4 %all-to-all-start.7 = ((bf16[4,12,2048]{2,1,0:T(8,128)(2,1)}), bf16[4,12,2048]{2,1,0:T(8,128)(2,1)S(1)}, u32[]{:S(2)}, u32[]{:S(2)}) async-start(bf16[4,12,2048]{2,1,0:T(8,128)(2,1)} %reshape.561), calls=%async_computation.7 | async-start | bytes 524288 | tf_op jit(solution)/shard_map/all_to_all | solution.py:76
  166.8 9.4 %all-to-all-start.2 = ((bf16[4,12,2048]{2,1,0:T(8,128)(2,1)}), bf16[4,12,2048]{2,1,0:T(8,128)(2,1)S(1)}, u32[]{:S(2)}, u32[]{:S(2)}) async-start(bf16[4,12,2048]{2,1,0:T(8,128)(2,1)} %reshape.554), calls=%async_computation.2 | async-start | bytes 524288 | tf_op jit(solution)/shard_map/all_to_all | solution.py:75
  170.3 65.5 %reduce-scatter.2.cloned.1.call-start = ((), (), s32[]{:S(2)}) async-start(), calls=%async_computation.9 | async-start | bytes 3604480 | tf_op jit(solution)/shard_map/reduce_scatter | solution.py:109
  176.3 2.1 copy-start.1
  176.3 2.6 %copy-start.12 = (f32[48]{0:T(128)S(1)}, f32[48]{0:T(128)}, u32[]{:S(2)}) copy-start(f32[48]{0:T(128)} %reshape.567) | copy-start | bytes 580
  182.5 8.9 %copy-start.4 = (bf16[64,2048]{1,0:T(8,128)(2,1)S(1)}, bf16[64,2048]{1,0:T(8,128)(2,1)}, u32[]{:S(2)}) copy-start(bf16[64,2048]{1,0:T(8,128)(2,1)} %copy-done.3) | copy-start | bytes 786436
  182.5 9.5 %copy-start.6 = (bf16[64,2048]{1,0:T(8,128)(2,1)S(1)}, bf16[64,2048]{1,0:T(8,128)(2,1)}, u32[]{:S(2)}) copy-start(bf16[64,2048]{1,0:T(8,128)(2,1)} %copy-done.5) | copy-start | bytes 786436
  (2 other events, 2.1 us)
Sparse Core Ops, SparseCore 0:
  9.6 37.4 all-gather.6
  48.6 33.8 all-gather.8
  84.0 33.7 all-gather.10
  181.3 54.3 reduce-scatter.1
where the time goes:
time: 243 us; the launch traced here: 242 us
  waiting for transfers between devices  166 us (68%)
  starting transfers between devices  28 us (12%)
  matrix products  14.2 us (6%)
  between operations  14.2 us (6%)
  blocking collectives  8.39 us (3%)
  local copies, waits for them, and re-layouts  8.09 us (3%)
  other arithmetic  3.92 us (2%)
    reduce_scatter x1, waiting for transfers between devices, local(): lax.psum_scatter(grad_total, 'dp', scatter_dimension=1, tiled=True)  42.8 us
    all_gather x1, waiting for transfers between devices, local(): lax.all_gather(w_up[0], 'dp', axis=1, tiled=True)  33.5 us
    all_gather x1, waiting for transfers between devices, local(): lax.all_gather(w_down[0], 'dp', axis=1, tiled=True)  33.4 us
    all_gather x1, waiting for transfers between devices, local(): lax.all_gather(w_gate[0], 'dp', axis=1, tiled=True)  24.1 us
    all_to_all x2, waiting for transfers between devices, local(): lax.all_to_all(send_cot, 'expert', split_axis=0, concat_axis=0, tiled=True)  10.9 us
    all_to_all x2, waiting for transfers between devices, local(): lax.all_to_all(send_tok, 'expert', split_axis=0, concat_axis=0, tiled=True)  9.79 us
    all_to_all x1, blocking collectives, local(): lax.all_to_all(partial_value, 'expert', split_axis=0, concat_axis=0, tile...  8.39 us
    all_to_all x2, starting transfers between devices, local(): lax.all_to_all(send_tok, 'expert', split_axis=0, concat_axis=0, tiled=True)  7.67 us
  transfers between devices with their start and end apart: 12, of which 11 were waited for; matrix products, arithmetic and copies ran while one was open for 6% of the time, Pallas kernels for 0%

commit v1 on v0

--- a/solution.py
+++ b/solution.py
@@ -1,3 +1,4 @@
+import functools
 import jax
 import jax.numpy as jnp
 from jax import lax
@@ -5,6 +6,13 @@
 
 SPLIT = 4
 CAP = 12
+
+
+def _lead_columns(a0, dev_axis):
+    return jnp.concatenate(lax.all_gather(a0, dev_axis), axis=1)
+
+
+order_domain = functools.partial(_lead_columns, dev_axis="dp")
 
 
 def shifted_2(shard, axis, by):
@@ -23,7 +31,7 @@
     gains = norm_gain[0]
     gate_local, up_local, down_local = (
         lax.all_gather(w_gate[0], "dp", axis=1, tiled=True),
-        lax.all_gather(w_up[0], "dp", axis=1, tiled=True),
+        order_domain(w_up[0]),
         lax.all_gather(w_down[0], "dp", axis=1, tiled=True),
     )
     hid_rows = gate_local.shape[0]

time: 243 us -> 243 us (level)
    all_gather x1, waiting for transfers between devices: 24.1 us -> 33.9 us  [local(): lax.all_gather(w_gate[0], 'dp', axis=1, tiled=True)]
    all_gather x1, waiting for transfers between devices: 33.5 us -> 24 us  [_lead_columns(): return jnp.concatenate(lax.all_gather(a0, dev_axis), axis=1)]
  transfers between devices with their start and end apart: 12 -> 12, of which waited for: 11 -> 10; matrix products, arithmetic and copies ran while one was open for 6% -> 7% of each run, Pallas kernels for 0% -> 0%
where the time goes in v1:
time: 243 us; the launch traced here: 242 us
  waiting for transfers between devices  164 us (67%)
  starting transfers between devices  28.7 us (12%)
  between operations  14.2 us (6%)
  matrix products  13 us (5%)
  local copies, waits for them, and re-layouts  10.2 us (4%)
  blocking collectives  8.39 us (3%)
  other arithmetic  3.92 us (2%)
    reduce_scatter x1, waiting for transfers between devices, local(): lax.psum_scatter(grad_total, 'dp', scatter_dimension=1, tiled=True)  43.3 us
    all_gather x1, waiting for transfers between devices, local(): lax.all_gather(w_gate[0], 'dp', axis=1, tiled=True)  33.9 us
    all_gather x1, waiting for transfers between devices, local(): lax.all_gather(w_down[0], 'dp', axis=1, tiled=True)  32.8 us
    all_gather x1, waiting for transfers between devices, _lead_columns(): return jnp.concatenate(lax.all_gather(a0, dev_axis), axis=1)  24 us
    all_to_all x2, waiting for transfers between devices, local(): lax.all_to_all(send_cot, 'expert', split_axis=0, concat_axis=0, tiled=True)  11 us
    all_to_all x1, blocking collectives, local(): lax.all_to_all(partial_value, 'expert', split_axis=0, concat_axis=0, tile...  8.39 us
    all_to_all x2, waiting for transfers between devices, local(): lax.all_to_all(send_tok, 'expert', split_axis=0, concat_axis=0, tiled=True)  8.1 us
    all_to_all x2, starting transfers between devices, local(): lax.all_to_all(send_tok, 'expert', split_axis=0, concat_axis=0, tiled=True)  7.67 us
  transfers between devices with their start and end apart: 12, of which 10 were waited for; matrix products, arithmetic and copies ran while one was open for 7% of the time, Pallas kernels for 0%

profile of v1, /device:TPU:0, one launch (start us, length us, event | category | flops | bytes accessed | tf_op | source)
XLA Modules:
  0.0 242.4 jit_solution(4790391423137975508)
XLA Ops:
  12.7 4.3 %all-to-all-start = ((bf16[4,12,2048]{2,1,0:T(8,128)(2,1)}), bf16[4,12,2048]{2,1,0:T(8,128)(2,1)S(1)}, u32[]{:S(2)}, u32[]{:S(2)}) async-start(bf16[4,12,2048]{2,1,0:T(8,128)(2,1)} %reshape.556), calls=%async_computation | async-start | bytes 524288 | tf_op jit(solution)/shard_map/all_to_all | solution.py:83
  17.7 5.3 %all-to-all-done = bf16[4,12,2048]{2,1,0:T(8,128)(2,1)S(1)} async-done(((bf16[4,12,2048]{2,1,0:T(8,128)(2,1)}), bf16[4,12,2048]{2,1,0:T(8,128)(2,1)S(1)}, u32[]{:S(2)}, u32[]{:S(2)}) %all-to-all-start) | async-done | bytes 196640 | tf_op jit(solution)/shard_map/all_to_all | solution.py:83
  23.0 24.0 %all-gather.6.cloned.1.call-done = bf16[4,352,512]{2,1,0:T(8,128)(2,1)} async-done(((bf16[1,352,512]{2,1,0:T(8,128)(2,1)}), bf16[4,352,512]{2,1,0:T(8,128)(2,1)}) %all-gather.6.cloned.1.call-update) | async-done | bytes 1441808 | tf_op jit(solution)/shard_map/all_gather | solution.py:12
  47.0 1.5 copy.22
  48.6 33.9 %all-gather.8.cloned.1.call-done = bf16[1,352,2048]{2,1,0:T(8,128)(2,1)} async-done(((bf16[1,352,512]{2,1,0:T(8,128)(2,1)}), bf16[1,352,2048]{2,1,0:T(8,128)(2,1)}) %all-gather.8.cloned.1.call-update) | async-done | bytes 1441808 | tf_op jit(solution)/shard_map/all_gather | solution.py:33
  82.5 1.9 fusion.7
  85.0 32.8 %all-gather.10.cloned.1.call-done = bf16[1,352,2048]{2,1,0:T(8,128)(2,1)} async-done(((bf16[1,352,512]{2,1,0:T(8,128)(2,1)}), bf16[1,352,2048]{2,1,0:T(8,128)(2,1)}) %all-gather.10.cloned.1.call-update) | async-done | bytes 1441808 | tf_op jit(solution)/shard_map/all_gather | solution.py:35
  117.8 1.7 convolution_convert_fusion.1
  120.3 3.4 %all-to-all-start.1 = ((bf16[4,12,2048]{2,1,0:T(8,128)(2,1)}), bf16[4,12,2048]{2,1,0:T(8,128)(2,1)S(1)}, u32[]{:S(2)}, u32[]{:S(2)}) async-start(bf16[4,12,2048]{2,1,0:T(8,128)(2,1)} %reshape.560), calls=%async_computation.1 | async-start | bytes 524288 | tf_op jit(solution)/shard_map/all_to_all | solution.py:108
  123.9 5.8 %all-to-all-done.1 = bf16[4,12,2048]{2,1,0:T(8,128)(2,1)S(1)} async-done(((bf16[4,12,2048]{2,1,0:T(8,128)(2,1)}), bf16[4,12,2048]{2,1,0:T(8,128)(2,1)S(1)}, u32[]{:S(2)}, u32[]{:S(2)}) %all-to-all-start.1) | async-done | bytes 196640 | tf_op jit(solution)/shard_map/all_to_all | solution.py:108
  130.3 3.2 %all-to-all-start.4 = ((bf16[4,1,12]{2,1,0:T(2,128)(2,1)}), bf16[4,1,12]{2,1,0:T(2,128)(2,1)S(1)}, u32[]{:S(2)}, u32[]{:S(2)}) async-start(bf16[4,1,12]{2,1,0:T(2,128)(2,1)} %reshape.565), calls=%async_computation.4 | async-start | bytes 4096 | tf_op jit(solution)/shard_map/all_to_all | solution.py:85
  134.2 3.0 %all-to-all-done.4 = bf16[4,1,12]{2,1,0:T(2,128)(2,1)S(1)} async-done(((bf16[4,1,12]{2,1,0:T(2,128)(2,1)}), bf16[4,1,12]{2,1,0:T(2,128)(2,1)S(1)}, u32[]{:S(2)}, u32[]{:S(2)}) %all-to-all-start.4) | async-done | bytes 128 | tf_op jit(solution)/shard_map/all_to_all | solution.py:85
  137.8 3.2 %all-to-all-start.6 = ((bf16[4,1,12]{2,1,0:T(2,128)(2,1)}), bf16[4,1,12]{2,1,0:T(2,128)(2,1)S(1)}, u32[]{:S(2)}, u32[]{:S(2)}) async-start(bf16[4,1,12]{2,1,0:T(2,128)(2,1)} %reshape.568), calls=%async_computation.6 | async-start | bytes 4096 | tf_op jit(solution)/shard_map/all_to_all | solution.py:85
  141.0 4.2 %collective-permute-start = (bf16[64,2048]{1,0:T(8,128)(2,1)S(1)}, bf16[64,2048]{1,0:T(8,128)(2,1)}, u32[]{:S(2)}, u32[]{:S(2)}) collective-permute-start(bf16[64,2048]{1,0:T(8,128)(2,1)S(1)} %fusion), channel_id=1, source_target_pairs={{0,16},{1,17},{2,18},{3,19},{4,20},{5,21},{6,22},{7,23},{8,24},{9,... | collective-permute-start | bytes 786440 | tf_op jit(solution)/shard_map/ppermute | solution.py:21
  145.9 3.4 %all-to-all-start.5 = ((bf16[4,12,2048]{2,1,0:T(8,128)(2,1)}), bf16[4,12,2048]{2,1,0:T(8,128)(2,1)S(1)}, u32[]{:S(2)}, u32[]{:S(2)}) async-start(bf16[4,12,2048]{2,1,0:T(8,128)(2,1)} %reshape.566), calls=%async_computation.5 | async-start | bytes 524288 | tf_op jit(solution)/shard_map/all_to_all | solution.py:84
  149.5 5.8 %all-to-all-done.5 = bf16[4,12,2048]{2,1,0:T(8,128)(2,1)S(1)} async-done(((bf16[4,12,2048]{2,1,0:T(8,128)(2,1)}), bf16[4,12,2048]{2,1,0:T(8,128)(2,1)S(1)}, u32[]{:S(2)}, u32[]{:S(2)}) %all-to-all-start.5) | async-done | bytes 196640 | tf_op jit(solution)/shard_map/all_to_all | solution.py:84
  156.0 3.4 %all-to-all-start.7 = ((bf16[4,12,2048]{2,1,0:T(8,128)(2,1)}), bf16[4,12,2048]{2,1,0:T(8,128)(2,1)S(1)}, u32[]{:S(2)}, u32[]{:S(2)}) async-start(bf16[4,12,2048]{2,1,0:T(8,128)(2,1)} %reshape.569), calls=%async_computation.7 | async-start | bytes 524288 | tf_op jit(solution)/shard_map/all_to_all | solution.py:84
  160.2 5.2 %all-to-all-done.7 = bf16[4,12,2048]{2,1,0:T(8,128)(2,1)S(1)} async-done(((bf16[4,12,2048]{2,1,0:T(8,128)(2,1)}), bf16[4,12,2048]{2,1,0:T(8,128)(2,1)S(1)}, u32[]{:S(2)}, u32[]{:S(2)}) %all-to-all-start.7) | async-done | bytes 196640 | tf_op jit(solution)/shard_map/all_to_all | solution.py:84
  167.4 3.4 %all-to-all-start.2 = ((bf16[4,12,2048]{2,1,0:T(8,128)(2,1)}), bf16[4,12,2048]{2,1,0:T(8,128)(2,1)S(1)}, u32[]{:S(2)}, u32[]{:S(2)}) async-start(bf16[4,12,2048]{2,1,0:T(8,128)(2,1)} %reshape.562), calls=%async_computation.2 | async-start | bytes 524288 | tf_op jit(solution)/shard_map/all_to_all | solution.py:83
  170.9 3.1 %fusion.29 = f32[352,2048]{1,0:T(8,128)} fusion(bf16[48,2048]{1,0:T(8,128)(2,1)S(1)} %reshape.567, bf16[48,352]{1,0:T(8,128)(2,1)} %copy-done.9, f32[48]{0:T(128)S(1)} %reshape.574), kind=kOutput, calls=%fused_computation.48 | convolution fusion | flops 69256704 | bytes 3114176 | tf_op jit(solution)/shard_map/dot_general | solution.py:103
  174.0 2.8 %all-to-all-done.2 = bf16[4,12,2048]{2,1,0:T(8,128)(2,1)S(1)} async-done(((bf16[4,12,2048]{2,1,0:T(8,128)(2,1)}), bf16[4,12,2048]{2,1,0:T(8,128)(2,1)S(1)}, u32[]{:S(2)}, u32[]{:S(2)}) %all-to-all-start.2) | async-done | bytes 196640 | tf_op jit(solution)/shard_map/all_to_all | solution.py:83
  178.7 2.2 convolution_add_fusion
  182.7 8.4 %all_to_all.42 = bf16[4,12,2048]{2,1,0:T(8,128)(2,1)S(1)} all-to-all(bf16[4,12,2048]{2,1,0:T(8,128)(2,1)S(1)} %reshape.564), channel_id=1, replica_groups=mesh['section'=2,'expert'=4,'dp'=4] {'expert'}, dimensions={0} | all-to-all | bytes 393216 | tf_op jit(solution)/shard_map/all_to_all | solution.py:108
  192.6 43.3 %reduce-scatter.2.cloned.1.call-done = f32[352,512]{1,0:T(8,128)} async-done(((f32[352,2048]{1,0:T(8,128)}), f32[352,512]{1,0:T(8,128)}) %reduce-scatter.2.cloned.1.call-update) | async-done | bytes 720912 | tf_op jit(solution)/shard_map/reduce_scatter | solution.py:117
  (89 shorter events, 18.9 us)
Async XLA Ops:
  7.2 10.1 %copy-start.11 = (s32[1,2,64,6]{2,1,3,0:T(2,128)S(1)}, s32[1,2,64,6]{2,1,3,0:T(2,128)}, u32[]{:S(2)}) copy-start(s32[1,2,64,6]{2,1,3,0:T(2,128)} %param.11) | copy-start | bytes 9220
  7.2 4.5 %copy-start.3 = (bf16[1,64,2048]{2,1,0:T(8,128)(2,1)S(1)}, bf16[1,64,2048]{2,1,0:T(8,128)(2,1)}, u32[]{:S(2)}) copy-start(bf16[1,64,2048]{2,1,0:T(8,128)(2,1)} %param.9) | copy-start | bytes 786436
  7.2 4.5 %copy-start.14 = (f32[1,2048]{1,0:T(1,128)S(1)}, f32[1,2048]{1,0:T(1,128)}, u32[]{:S(2)}) copy-start(f32[1,2048]{1,0:T(1,128)} %param.14) | copy-start | bytes 24580
  7.2 10.1 %copy-start.12 = (bf16[1,2,64,6]{2,1,3,0:T(2,128)(2,1)S(1)}, bf16[1,2,64,6]{2,1,3,0:T(2,128)(2,1)}, u32[]{:S(2)}) copy-start(bf16[1,2,64,6]{2,1,3,0:T(2,128)(2,1)} %param.12) | copy-start | bytes 4612
  7.2 39.8 %all-gather.6.cloned.1.call-start = ((), (), s32[]{:S(2)}) async-start(), calls=%async_computation.9 | async-start | bytes 1802240 | tf_op jit(solution)/shard_map/all_gather | solution.py:12
  7.9 74.5 %all-gather.8.cloned.1.call-start = ((), (), s32[]{:S(2)}) async-start(), calls=%async_computation.11 | async-start | bytes 1802240 | tf_op jit(solution)/shard_map/all_gather | solution.py:33
  8.7 109.1 %all-gather.10.cloned.1.call-start = ((), (), s32[]{:S(2)}) async-start(), calls=%async_computation.12 | async-start | bytes 1802240 | tf_op jit(solution)/shard_map/all_gather | solution.py:35
  12.7 10.3 %all-to-all-start = ((bf16[4,12,2048]{2,1,0:T(8,128)(2,1)}), bf16[4,12,2048]{2,1,0:T(8,128)(2,1)S(1)}, u32[]{:S(2)}, u32[]{:S(2)}) async-start(bf16[4,12,2048]{2,1,0:T(8,128)(2,1)} %reshape.556), calls=%async_computation | async-start | bytes 524288 | tf_op jit(solution)/shard_map/all_to_all | solution.py:83
  85.0 35.3 %copy-start.9 = (bf16[48,352]{1,0:T(8,128)(2,1)}, bf16[48,352]{1,0:T(8,128)(2,1)S(1)}, u32[]{:S(2)}) copy-start(bf16[48,352]{1,0:T(8,128)(2,1)S(1)} %fusion.9) | copy-start | bytes 101380
  85.0 38.8 %copy-start.8 = (bf16[1,2,64,2048]{3,2,1,0:T(8,128)(2,1)S(1)}, bf16[1,2,64,2048]{3,2,1,0:T(8,128)(2,1)}, u32[]{:S(2)}) copy-start(bf16[1,2,64,2048]{3,2,1,0:T(8,128)(2,1)} %param.13) | copy-start | bytes 1572868
  120.3 9.4 %all-to-all-start.1 = ((bf16[4,12,2048]{2,1,0:T(8,128)(2,1)}), bf16[4,12,2048]{2,1,0:T(8,128)(2,1)S(1)}, u32[]{:S(2)}, u32[]{:S(2)}) async-start(bf16[4,12,2048]{2,1,0:T(8,128)(2,1)} %reshape.560), calls=%async_computation.1 | async-start | bytes 524288 | tf_op jit(solution)/shard_map/all_to_all | solution.py:108
  130.3 6.9 %all-to-all-start.4 = ((bf16[4,1,12]{2,1,0:T(2,128)(2,1)}), bf16[4,1,12]{2,1,0:T(2,128)(2,1)S(1)}, u32[]{:S(2)}, u32[]{:S(2)}) async-start(bf16[4,1,12]{2,1,0:T(2,128)(2,1)} %reshape.565), calls=%async_computation.4 | async-start | bytes 4096 | tf_op jit(solution)/shard_map/all_to_all | solution.py:85
  134.2 31.3 %copy-start.6 = (bf16[64,2048]{1,0:T(8,128)(2,1)}, bf16[64,2048]{1,0:T(8,128)(2,1)S(1)}, u32[]{:S(2)}) copy-start(bf16[64,2048]{1,0:T(8,128)(2,1)S(1)} %fusion) | copy-start | bytes 786436
  137.8 7.4 %all-to-all-start.6 = ((bf16[4,1,12]{2,1,0:T(2,128)(2,1)}), bf16[4,1,12]{2,1,0:T(2,128)(2,1)S(1)}, u32[]{:S(2)}, u32[]{:S(2)}) async-start(bf16[4,1,12]{2,1,0:T(2,128)(2,1)} %reshape.568), calls=%async_computation.6 | async-start | bytes 4096 | tf_op jit(solution)/shard_map/all_to_all | solution.py:85
  141.0 24.5 %copy-start.10 = (bf16[1,64,2048]{2,1,0:T(8,128)(2,1)S(1)}, bf16[1,64,2048]{2,1,0:T(8,128)(2,1)}, u32[]{:S(2)}) copy-start(bf16[1,64,2048]{2,1,0:T(8,128)(2,1)} %param.10) | copy-start | bytes 786436
  141.0 24.5 %collective-permute-start = (bf16[64,2048]{1,0:T(8,128)(2,1)S(1)}, bf16[64,2048]{1,0:T(8,128)(2,1)}, u32[]{:S(2)}, u32[]{:S(2)}) collective-permute-start(bf16[64,2048]{1,0:T(8,128)(2,1)S(1)} %fusion), channel_id=1, source_target_pairs={{0,16},{1,17},{2,18},{3,19},{4,20},{5,21},{6,22},{7,23},{8,24},{9,... | collective-permute-start | bytes 786440 | tf_op jit(solution)/shard_map/ppermute | solution.py:21
  145.9 9.4 %all-to-all-start.5 = ((bf16[4,12,2048]{2,1,0:T(8,128)(2,1)}), bf16[4,12,2048]{2,1,0:T(8,128)(2,1)S(1)}, u32[]{:S(2)}, u32[]{:S(2)}) async-start(bf16[4,12,2048]{2,1,0:T(8,128)(2,1)} %reshape.566), calls=%async_computation.5 | async-start | bytes 524288 | tf_op jit(solution)/shard_map/all_to_all | solution.py:84
  156.0 9.4 %all-to-all-start.7 = ((bf16[4,12,2048]{2,1,0:T(8,128)(2,1)}), bf16[4,12,2048]{2,1,0:T(8,128)(2,1)S(1)}, u32[]{:S(2)}, u32[]{:S(2)}) async-start(bf16[4,12,2048]{2,1,0:T(8,128)(2,1)} %reshape.569), calls=%async_computation.7 | async-start | bytes 524288 | tf_op jit(solution)/shard_map/all_to_all | solution.py:84
  167.4 9.4 %all-to-all-start.2 = ((bf16[4,12,2048]{2,1,0:T(8,128)(2,1)}), bf16[4,12,2048]{2,1,0:T(8,128)(2,1)S(1)}, u32[]{:S(2)}, u32[]{:S(2)}) async-start(bf16[4,12,2048]{2,1,0:T(8,128)(2,1)} %reshape.562), calls=%async_computation.2 | async-start | bytes 524288 | tf_op jit(solution)/shard_map/all_to_all | solution.py:83
  170.8 6.0 %copy-start.2 = (bf16[1,352,2048]{2,1,0:T(8,128)(2,1)S(1)}, bf16[1,352,2048]{2,1,0:T(8,128)(2,1)}, u32[]{:S(2)}) copy-start(bf16[1,352,2048]{2,1,0:T(8,128)(2,1)} %all-gather.8.cloned.1.call-done) | copy-start | bytes 4325380
  170.8 65.0 %reduce-scatter.2.cloned.1.call-start = ((), (), s32[]{:S(2)}) async-start(), calls=%async_computation.10 | async-start | bytes 3604480 | tf_op jit(solution)/shard_map/reduce_scatter | solution.py:117
  176.8 1.8 copy-start
  182.2 8.9 %copy-start.5 = (bf16[64,2048]{1,0:T(8,128)(2,1)S(1)}, bf16[64,2048]{1,0:T(8,128)(2,1)}, u32[]{:S(2)}) copy-start(bf16[64,2048]{1,0:T(8,128)(2,1)} %copy-done.4) | copy-start | bytes 786436
  182.2 9.5 %copy-start.7 = (bf16[64,2048]{1,0:T(8,128)(2,1)S(1)}, bf16[64,2048]{1,0:T(8,128)(2,1)}, u32[]{:S(2)}) copy-start(bf16[64,2048]{1,0:T(8,128)(2,1)} %copy-done.6) | copy-start | bytes 786436
  (3 other events, 3.9 us)
Sparse Core Ops, SparseCore 0:
  9.6 37.4 all-gather.5
  48.6 33.8 all-gather.7
  84.0 33.7 all-gather.9
  181.0 54.8 reduce-scatter.1
